TPU v7x, 32 devices: a whole 2x2x4 slice. The times are simulated.
32 devices in a mesh: seq: 16 (over z, x, core), fsdp: 2 (over y).
Axes of the slice: x: 2, y: 2, z: 4, core: 2. Of those that a mesh axis runs over, the one named last changes fastest.
Arguments:
- queries: bfloat16 [8192, 2048], P(('seq', 'fsdp')), may hold values from -150 to 150
- key_rotated_rows: bfloat16 [8192, 1024], P(('seq', 'fsdp')), may hold values from -5 to 5
- values: bfloat16 [8192, 1024], P(('seq', 'fsdp')), may hold values from -6 to 6
- out_weight: bfloat16 [2048, 5376], P('seq', 'fsdp'), may hold values from -0.125 to 0.125
- residual: bfloat16 [8192, 5376], P(('seq', 'fsdp')), may hold values from -6 to 6
- norm_gain: float32 [5376], replicated, may hold values from 0.25 to 1.75
- doc_lengths: int32 [8], replicated, may hold values from 1 to 2048, 8192 in all
Outputs:
- output: bfloat16 [8192, 5376], P(('seq', 'fsdp'))
All inputs are finite; a program needn't handle non-finite values.
Results may differ from a plain program's by a relative error of at most 0.007.
Values may be sent and summed in bfloat16 or wider, within the bound.
No kernel may reach another device: no remote copies, remote signals or barrier semaphores. Data moves between devices by JAX's collectives and lax.ppermute only.
A program may use at most 128 MiB of HBM per device.

v0:
```python
import jax
import jax.numpy as jnp
from jax import lax
from jax.sharding import PartitionSpec as P

QUERY_HEADS = 16
KEY_VALUE_HEADS = 8
HEAD_SIZE = 128
WINDOW_TOKENS = 1024
QSCALE = 168


def from_behind(value, axis, by):
    count = lax.axis_size(axis)
    pairs = [(i, i + by) for i in range(count) if 0 <= i + by < count]
    return lax.ppermute(value, axis, pairs)


def doc_index(positions, starts):
    return jnp.sum((starts[None, :] <= positions[:, None]).astype(jnp.int32), axis=1) - 1


def shards(queries, key_rotated_rows, values, out_weight, residual, norm_gain, doc_lengths):
    token_rows = queries.shape[0]
    behind = WINDOW_TOKENS // token_rows
    queries_per_group = QUERY_HEADS // KEY_VALUE_HEADS
    scaling = QSCALE ** (-0.5)
    token_offset = lax.axis_index(("seq", "fsdp")) * token_rows
    starts = jnp.cumsum(doc_lengths) - doc_lengths
    earlier = []
    carried = (key_rotated_rows, values)
    for distance in range(behind):
        carried = from_behind((carried[0], carried[1]), ("seq", "fsdp"), 1)
        earlier.append(carried)
    ordered = earlier[::-1] + [(key_rotated_rows, values)]
    key_gathered = jnp.concatenate([paired[0] for paired in ordered], axis=0)
    value_gathered = jnp.concatenate([paired[1] for paired in ordered], axis=0)
    total_count = key_gathered.shape[0]
    q_pos = token_offset + jnp.arange(token_rows, dtype=jnp.int32)
    k_pos = token_offset - behind * token_rows + jnp.arange(total_count, dtype=jnp.int32)
    q_doc = doc_index(q_pos, starts)
    k_doc = doc_index(k_pos, starts)
    lag = q_pos[:, None] - k_pos[None, :]
    allowed = (
        (q_doc[:, None] == k_doc[None, :])
        & (lag >= 0)
        & (lag < WINDOW_TOKENS)
        & (k_pos[None, :] >= 0)
    )
    last_pos = k_pos[token_rows - 1 :: token_rows]
    live = (last_pos >= 0) & (doc_index(last_pos, starts) == q_doc[0])
    live = jnp.concatenate([live[:-1], jnp.ones((1,), dtype=bool)])
    query_head_rows = queries.reshape(
        token_rows, KEY_VALUE_HEADS, queries_per_group * HEAD_SIZE
    ).transpose(1, 0, 2)
    key_head_rows = key_gathered.reshape(total_count, KEY_VALUE_HEADS, HEAD_SIZE).transpose(1, 0, 2)
    value_head_rows = value_gathered.reshape(total_count, KEY_VALUE_HEADS, HEAD_SIZE).transpose(
        1, 0, 2
    )

    def attend(operands):
        q_head, k_head, v_head = operands
        q_head = q_head.reshape(token_rows, queries_per_group, HEAD_SIZE)
        scores = jnp.einsum("qgd,kd->gqk", q_head, k_head, preferred_element_type=jnp.float32)
        scores = jnp.where(allowed[None], scores * scaling, -jnp.inf)
        peak = jnp.max(scores, axis=-1, keepdims=True)
        expon = jnp.exp(scores - peak)
        probs = (expon / jnp.sum(expon, axis=-1, keepdims=True)).astype(jnp.bfloat16)
        mixed = jnp.einsum("gqk,kd->qgd", probs, v_head, preferred_element_type=jnp.float32)
        return mixed.reshape(token_rows, queries_per_group * HEAD_SIZE)

    heads_out = lax.map(attend, (query_head_rows, key_head_rows, value_head_rows))
    attended = (
        heads_out.transpose(1, 0, 2)
        .reshape(token_rows, QUERY_HEADS * HEAD_SIZE)
        .astype(jnp.bfloat16)
    )
    widened = lax.all_gather(out_weight, "fsdp", axis=1, tiled=True)
    projected = jnp.dot(
        attended,
        lax.all_gather(widened, "seq", axis=0, tiled=True),
        preferred_element_type=jnp.float32,
    )
    meansq = jnp.mean(projected * projected, axis=-1, keepdims=True)
    output = residual.astype(jnp.float32) + norm_gain * projected * lax.rsqrt(meansq + 1e-06)
    return output.astype(jnp.bfloat16)


def solution(mesh):
    in_specs = (
        P(("seq", "fsdp"), None),
        P(("seq", "fsdp"), None),
        P(("seq", "fsdp"), None),
        P("seq", "fsdp"),
        P(("seq", "fsdp"), None),
        P(),
        P(),
    )
    out_specs = P(("seq", "fsdp"), None)
    return jax.shard_map(shards, mesh=mesh, in_specs=in_specs, out_specs=out_specs, check_vma=False)
```

profile of v0, /device:TPU:8, one launch (start us, length us, event | category | flops | bytes accessed | tf_op | source)
XLA Modules:
  0.0 247.7 jit_solution(636366835698399091)
XLA Ops:
  7.3 27.7 %all-gather.3.cloned.1.call-done = bf16[128,5376]{1,0:T(8,128)(2,1)} async-done(((bf16[128,2688]{1,0:T(8,128)(2,1)}), bf16[128,5376]{1,0:T(8,128)(2,1)}) %all-gather.3.cloned.1.call-update) | async-done | bytes 1376272 | tf_op jit(solution)/shard_map/all_gather | solution.py:78
  35.1 2.5 collective-permute-start
  37.5 1.2 copy.20
  38.8 2.7 %collective-permute-start.4 = (bf16[256,1024]{0,1:T(8,128)(2,1)S(1)}, bf16[256,1024]{0,1:T(8,128)(2,1)S(1)}, u32[]{:S(2)}, u32[]{:S(2)}) collective-permute-start(bf16[256,1024]{0,1:T(8,128)(2,1)S(1)} %copy.20), channel_id=1, source_target_pairs={{0,1},{1,2},{2,3},{3,4},{4,5},{5,6},{6,7},{7,8},{8,9},{9,10},{10,1... | collective-permute-start | bytes 1572872 | tf_op jit(solution)/shard_map/ppermute | solution.py:16
  41.5 9.1 %collective-permute-done = bf16[256,1024]{1,0:T(8,128)(2,1)S(1)} collective-permute-done((bf16[256,1024]{1,0:T(8,128)(2,1)}, bf16[256,1024]{1,0:T(8,128)(2,1)S(1)}, u32[]{:S(2)}, u32[]{:S(2)}) %collective-permute-start) | collective-permute-done | bytes 524320 | tf_op jit(solution)/shard_map/ppermute | solution.py:16
  50.5 3.9 %collective-permute-start.1 = (bf16[256,1024]{1,0:T(8,128)(2,1)S(1)}, bf16[256,1024]{1,0:T(8,128)(2,1)S(1)}, u32[]{:S(2)}, u32[]{:S(2)}) collective-permute-start(bf16[256,1024]{1,0:T(8,128)(2,1)S(1)} %collective-permute-done), channel_id=1, source_target_pairs={{0,1},{1,2},{2,3},{3,4},{4,5},{5,6},{6,7},{7,8},{8,9},{9,10},{10,1... | collective-permute-start | bytes 1572872 | tf_op jit(solution)/shard_map/ppermute | solution.py:16
  54.5 1.3 copy.22
  56.0 11.4 %collective-permute-done.4 = bf16[256,1024]{0,1:T(8,128)(2,1)S(1)} collective-permute-done((bf16[256,1024]{0,1:T(8,128)(2,1)S(1)}, bf16[256,1024]{0,1:T(8,128)(2,1)S(1)}, u32[]{:S(2)}, u32[]{:S(2)}) %collective-permute-start.4) | collective-permute-done | bytes 524320 | tf_op jit(solution)/shard_map/ppermute | solution.py:16
  67.4 1.9 collective-permute-start.5
  69.3 14.9 %collective-permute-done.1 = bf16[256,1024]{1,0:T(8,128)(2,1)S(1)} collective-permute-done((bf16[256,1024]{1,0:T(8,128)(2,1)S(1)}, bf16[256,1024]{1,0:T(8,128)(2,1)S(1)}, u32[]{:S(2)}, u32[]{:S(2)}) %collective-permute-start.1) | collective-permute-done | bytes 524320 | tf_op jit(solution)/shard_map/ppermute | solution.py:16
  84.2 1.9 collective-permute-start.2
  86.3 14.7 %collective-permute-done.5 = bf16[256,1024]{0,1:T(8,128)(2,1)S(1)} collective-permute-done((bf16[256,1024]{0,1:T(8,128)(2,1)S(1)}, bf16[256,1024]{0,1:T(8,128)(2,1)S(1)}, u32[]{:S(2)}, u32[]{:S(2)}) %collective-permute-start.5) | collective-permute-done | bytes 524320 | tf_op jit(solution)/shard_map/ppermute | solution.py:16
  101.1 1.9 collective-permute-start.6
  103.0 14.9 %collective-permute-done.2 = bf16[256,1024]{1,0:T(8,128)(2,1)S(1)} collective-permute-done((bf16[256,1024]{1,0:T(8,128)(2,1)S(1)}, bf16[256,1024]{1,0:T(8,128)(2,1)S(1)}, u32[]{:S(2)}, u32[]{:S(2)}) %collective-permute-start.2) | collective-permute-done | bytes 524320 | tf_op jit(solution)/shard_map/ppermute | solution.py:16
  117.9 1.9 collective-permute-start.3
  119.9 15.0 %collective-permute-done.6 = bf16[256,1024]{0,1:T(8,128)(2,1)} collective-permute-done((bf16[256,1024]{0,1:T(8,128)(2,1)S(1)}, bf16[256,1024]{0,1:T(8,128)(2,1)}, u32[]{:S(2)}, u32[]{:S(2)}) %collective-permute-start.6) | collective-permute-done | bytes 524320 | tf_op jit(solution)/shard_map/ppermute | solution.py:16
  134.9 1.9 collective-permute-start.7
  136.8 14.8 %collective-permute-done.3 = bf16[256,1024]{1,0:T(8,128)(2,1)S(1)} collective-permute-done((bf16[256,1024]{1,0:T(8,128)(2,1)S(1)}, bf16[256,1024]{1,0:T(8,128)(2,1)S(1)}, u32[]{:S(2)}, u32[]{:S(2)}) %collective-permute-start.3) | collective-permute-done | bytes 524320 | tf_op jit(solution)/shard_map/ppermute | solution.py:16
  151.7 1.1 constant_dynamic-update-slice_fusion.3
  154.0 2.7 %copy.19 = bf16[1280,1024]{0,1:T(8,128)(2,1)} copy(bf16[1280,1024]{1,0:T(8,128)(2,1)S(1)} %constant_dynamic-update-slice_fusion.1) | data formatting | bytes 5242880 | tf_op jit(solution)/shard_map/concatenate | solution.py:37
  156.7 11.9 %collective-permute-done.7 = bf16[256,1024]{0,1:T(8,128)(2,1)} collective-permute-done((bf16[256,1024]{0,1:T(8,128)(2,1)}, bf16[256,1024]{0,1:T(8,128)(2,1)}, u32[]{:S(2)}, u32[]{:S(2)}) %collective-permute-start.7) | collective-permute-done | bytes 524320 | tf_op jit(solution)/shard_map/ppermute | solution.py:16
  168.6 2.0 constant_dynamic-update-slice_fusion.10
  170.6 1.9 constant_dynamic-update-slice_fusion.9
  172.5 1.9 constant_dynamic-update-slice_fusion.8
  176.2 51.0 %while.11 = (s32[]{:T(128)}, bf16[8,256,256]{1,2,0:T(8,128)(2,1)S(1)}, bf16[8,1280,128]{1,2,0:T(8,128)(2,1)}, bf16[8,1280,128]{1,2,0:T(8,128)(2,1)}, bf16[8,256,...) while((s32[]{:T(128)}, ...), condition=%wide.region_6.7_spmd.clone, body=%wide.region_3.6_spmd.clone.sunk | while | flops 511511552 | bytes 2902901 | solution.py:72
  178.2 2.0 fusion.57
  180.2 2.3 fusion.58
  182.6 1.1 fusion.56
  184.6 2.0 fusion.57
  186.6 2.3 fusion.58
  188.9 1.1 fusion.56
  191.0 2.0 fusion.57
  192.9 2.3 fusion.58
  195.3 1.1 fusion.56
  197.4 2.0 fusion.57
  199.3 2.3 fusion.58
  201.7 1.1 fusion.56
  203.7 2.0 fusion.57
  205.7 2.3 fusion.58
  208.1 1.1 fusion.56
  210.1 2.0 fusion.57
  212.1 2.3 fusion.58
  216.5 2.0 fusion.57
  218.5 2.3 fusion.58
  222.9 2.0 fusion.57
  224.9 2.3 fusion.58
  227.3 11.0 %multiply_reduce_fusion = (f32[256]{0:T(256)S(1)}, f32[256,5376]{1,0:T(8,128)S(1)}) fusion(bf16[256,2048]{0,1:T(8,128)(2,1)S(1)} %bitcast.79, bf16[2048,5376]{1,0:T(8,128)(2,1)} %all-gather.5.cloned.1.call-done), kind=kOutput, calls=%fused_computation.29 | convolution fusion | flops 5639897088 | bytes 28574720 | tf_op jit(solution)/shard_map/dot_general | solution.py:79
  238.3 2.5 %add_convert_fusion = bf16[256,5376]{1,0:T(8,128)(2,1)} fusion(f32[256,5376]{1,0:T(8,128)S(1)} %get-tuple-element.106, bf16[256,5376]{1,0:T(8,128)(2,1)S(1)} %copy-done, f32[256]{0:T(256)S(1)} %add_rsqrt_fusion, f32[5376]{0:T(1024)S(1)} %copy-done.9), kind=kLoop, calls=%fused_computation.28 | loop fusion | flops 6881280 | bytes 11032576 | tf_op jit(solution)/shard_map/convert_element_type | solution.py:86
  (63 shorter events, 14.9 us)
Async XLA Ops:
  6.5 47.9 %copy-start.2 = (bf16[256,2048]{1,0:T(8,128)(2,1)S(1)}, bf16[256,2048]{1,0:T(8,128)(2,1)}, u32[]{:S(2)}) copy-start(bf16[256,2048]{1,0:T(8,128)(2,1)} %param.9) | copy-start | bytes 3145732
  6.5 49.2 %copy-start.10 = (s32[8]{0:T(128)S(1)}, s32[8]{0:T(128)}, u32[]{:S(2)}) copy-start(s32[8]{0:T(128)} %param.15) | copy-start | bytes 100
  6.5 28.5 %all-gather.3.cloned.1.call-start = ((), (), s32[]{:S(2)}) async-start(), calls=%async_computation | async-start | bytes 2064384 | tf_op jit(solution)/shard_map/all_gather | solution.py:78
  7.3 220.0 %all-gather.5.cloned.1.call-start = ((), (), s32[]{:S(2)}) async-start(), calls=%async_computation.1 | async-start | bytes 23396352 | tf_op jit(solution)/shard_map/all_gather | solution.py:81
  35.1 15.4 %collective-permute-start = (bf16[256,1024]{1,0:T(8,128)(2,1)}, bf16[256,1024]{1,0:T(8,128)(2,1)S(1)}, u32[]{:S(2)}, u32[]{:S(2)}) collective-permute-start(bf16[256,1024]{1,0:T(8,128)(2,1)} %param.11), channel_id=1, source_target_pairs={{0,1},{1,2},{2,3},{3,4},{4,5},{5,6},{6,7},{7,8},{8,9},{9,10},{10,1... | collective-permute-start | bytes 1572872 | tf_op jit(solution)/shard_map/ppermute | solution.py:16
  38.8 28.6 %collective-permute-start.4 = (bf16[256,1024]{0,1:T(8,128)(2,1)S(1)}, bf16[256,1024]{0,1:T(8,128)(2,1)S(1)}, u32[]{:S(2)}, u32[]{:S(2)}) collective-permute-start(bf16[256,1024]{0,1:T(8,128)(2,1)S(1)} %copy.20), channel_id=1, source_target_pairs={{0,1},{1,2},{2,3},{3,4},{4,5},{5,6},{6,7},{7,8},{8,9},{9,10},{10,1... | collective-permute-start | bytes 1572872 | tf_op jit(solution)/shard_map/ppermute | solution.py:16
  50.5 86.3 %copy-start.5 = (bf16[256,1024]{1,0:T(8,128)(2,1)}, bf16[256,1024]{1,0:T(8,128)(2,1)S(1)}, u32[]{:S(2)}) copy-start(bf16[256,1024]{1,0:T(8,128)(2,1)S(1)} %collective-permute-done) | copy-start | bytes 1572868
  50.5 33.7 %collective-permute-start.1 = (bf16[256,1024]{1,0:T(8,128)(2,1)S(1)}, bf16[256,1024]{1,0:T(8,128)(2,1)S(1)}, u32[]{:S(2)}, u32[]{:S(2)}) collective-permute-start(bf16[256,1024]{1,0:T(8,128)(2,1)S(1)} %collective-permute-done), channel_id=1, source_target_pairs={{0,1},{1,2},{2,3},{3,4},{4,5},{5,6},{6,7},{7,8},{8,9},{9,10},{10,1... | collective-permute-start | bytes 1572872 | tf_op jit(solution)/shard_map/ppermute | solution.py:16
  67.4 69.4 %copy-start.3 = (bf16[256,1024]{0,1:T(8,128)(2,1)}, bf16[256,1024]{0,1:T(8,128)(2,1)S(1)}, u32[]{:S(2)}) copy-start(bf16[256,1024]{0,1:T(8,128)(2,1)S(1)} %collective-permute-done.4) | copy-start | bytes 1572868
  67.4 33.7 %collective-permute-start.5 = (bf16[256,1024]{0,1:T(8,128)(2,1)S(1)}, bf16[256,1024]{0,1:T(8,128)(2,1)S(1)}, u32[]{:S(2)}, u32[]{:S(2)}) collective-permute-start(bf16[256,1024]{0,1:T(8,128)(2,1)S(1)} %collective-permute-done.4), channel_id=1, source_target_pairs={{0,1},{1,2},{2,3},{3,4},{4,5},{5,6},{6,7},{7,8},{8,9},{9,10},{10,1... | collective-permute-start | bytes 1572872 | tf_op jit(solution)/shard_map/ppermute | solution.py:16
  84.2 52.6 %copy-start.7 = (bf16[256,1024]{1,0:T(8,128)(2,1)}, bf16[256,1024]{1,0:T(8,128)(2,1)S(1)}, u32[]{:S(2)}) copy-start(bf16[256,1024]{1,0:T(8,128)(2,1)S(1)} %collective-permute-done.1) | copy-start | bytes 1572868
  84.2 33.7 %collective-permute-start.2 = (bf16[256,1024]{1,0:T(8,128)(2,1)S(1)}, bf16[256,1024]{1,0:T(8,128)(2,1)S(1)}, u32[]{:S(2)}, u32[]{:S(2)}) collective-permute-start(bf16[256,1024]{1,0:T(8,128)(2,1)S(1)} %collective-permute-done.1), channel_id=1, source_target_pairs={{0,1},{1,2},{2,3},{3,4},{4,5},{5,6},{6,7},{7,8},{8,9},{9,10},{10,1... | collective-permute-start | bytes 1572872 | tf_op jit(solution)/shard_map/ppermute | solution.py:16
  101.1 35.8 %copy-start.8 = (bf16[256,1024]{0,1:T(8,128)(2,1)}, bf16[256,1024]{0,1:T(8,128)(2,1)S(1)}, u32[]{:S(2)}) copy-start(bf16[256,1024]{0,1:T(8,128)(2,1)S(1)} %collective-permute-done.5) | copy-start | bytes 1572868
  101.1 33.8 %collective-permute-start.6 = (bf16[256,1024]{0,1:T(8,128)(2,1)S(1)}, bf16[256,1024]{0,1:T(8,128)(2,1)}, u32[]{:S(2)}, u32[]{:S(2)}) collective-permute-start(bf16[256,1024]{0,1:T(8,128)(2,1)S(1)} %collective-permute-done.5), channel_id=1, source_target_pairs={{0,1},{1,2},{2,3},{3,4},{4,5},{5,6},{6,7},{7,8},{8,9},{9,10},{10,1... | collective-permute-start | bytes 1572872 | tf_op jit(solution)/shard_map/ppermute | solution.py:16
  117.9 33.7 %collective-permute-start.3 = (bf16[256,1024]{1,0:T(8,128)(2,1)S(1)}, bf16[256,1024]{1,0:T(8,128)(2,1)S(1)}, u32[]{:S(2)}, u32[]{:S(2)}) collective-permute-start(bf16[256,1024]{1,0:T(8,128)(2,1)S(1)} %collective-permute-done.2), channel_id=1, source_target_pairs={{0,1},{1,2},{2,3},{3,4},{4,5},{5,6},{6,7},{7,8},{8,9},{9,10},{10,1... | collective-permute-start | bytes 1572872 | tf_op jit(solution)/shard_map/ppermute | solution.py:16
  134.9 33.7 %collective-permute-start.7 = (bf16[256,1024]{0,1:T(8,128)(2,1)}, bf16[256,1024]{0,1:T(8,128)(2,1)}, u32[]{:S(2)}, u32[]{:S(2)}) collective-permute-start(bf16[256,1024]{0,1:T(8,128)(2,1)} %collective-permute-done.6), channel_id=1, source_target_pairs={{0,1},{1,2},{2,3},{3,4},{4,5},{5,6},{6,7},{7,8},{8,9},{9,10},{10,1... | collective-permute-start | bytes 1572872 | tf_op jit(solution)/shard_map/ppermute | solution.py:16
  151.6 1.2 copy-start.6
  156.7 17.7 %copy-start.4 = (bf16[256,1024]{0,1:T(8,128)(2,1)S(1)}, bf16[256,1024]{0,1:T(8,128)(2,1)}, u32[]{:S(2)}) copy-start(bf16[256,1024]{0,1:T(8,128)(2,1)} %copy-done.3) | copy-start | bytes 1572868
  156.7 19.5 %copy-start.1 = (bf16[8,256,256]{1,2,0:T(8,128)(2,1)S(1)}, bf16[8,256,256]{1,2,0:T(8,128)(2,1)}, u32[]{:S(2)}) copy-start(bf16[8,256,256]{1,2,0:T(8,128)(2,1)} %custom-call.2) | copy-start | bytes 3145732
  227.3 11.0 %copy-start = (bf16[256,5376]{1,0:T(8,128)(2,1)S(1)}, bf16[256,5376]{1,0:T(8,128)(2,1)}, u32[]{:S(2)}) copy-start(bf16[256,5376]{1,0:T(8,128)(2,1)} %param.13) | copy-start | bytes 8257540
  227.3 11.0 %copy-start.9 = (f32[5376]{0:T(1024)S(1)}, f32[5376]{0:T(1024)}, u32[]{:S(2)}) copy-start(f32[5376]{0:T(1024)} %param.14) | copy-start | bytes 64516
Sparse Core Ops, SparseCore 0:
  8.9 26.1 all-gather.2
  36.6 113.6 all-gather.4
where the time goes:
time: 249 us; the launch traced here: 248 us
  waiting for transfers between devices  135 us (54%)
  matrix products  45.5 us (18%)
  local copies, waits for them, and re-layouts  22.7 us (9%)
  starting transfers between devices  18.6 us (7%)
  between operations  13.7 us (6%)
  other arithmetic  11.7 us (5%)
    ppermute x8, waiting for transfers between devices, from_behind(): return lax.ppermute(value, axis, pairs)  107 us
    all_gather x1, waiting for transfers between devices, shards(): widened = lax.all_gather(out_weight, 'fsdp', axis=1, tiled=True)  27.7 us
    dot_general x8, matrix products, attend(): jnp.einsum('gqk,kd->qgd', probs, v_head, preferred_element_type=jnp.float32)  18.7 us
    ppermute x8, starting transfers between devices, from_behind(): return lax.ppermute(value, axis, pairs)  18.6 us
    sub x8, matrix products, attend(): expon = jnp.exp(scores - peak)  15.8 us
    dot_general x1, matrix products, shards(): jnp.dot(attended, lax.all_gather(widened, 'seq', axis=0, tiled=True), pre...  11 us
    unnamed x32, local copies, waits for them, and re-layouts  10.5 us
    and x8, other arithmetic, shards(): (q_doc[:, None] == k_doc[None, :]) & (lag >= 0) & (lag < WINDOW_TOKENS)  8.73 us
  transfers between devices with their start and end apart: 10, of which 9 were waited for; matrix products, arithmetic and copies ran while one was open for 27% of the time, Pallas kernels for 0%

commit v1 on v0

--- a/solution.py
+++ b/solution.py
@@ -75,7 +75,7 @@
         .reshape(token_rows, QUERY_HEADS * HEAD_SIZE)
         .astype(jnp.bfloat16)
     )
-    widened = lax.all_gather(out_weight, "fsdp", axis=1, tiled=True)
+    widened = jnp.concatenate(lax.all_gather(out_weight, "fsdp"), axis=1)
     projected = jnp.dot(
         attended,
         lax.all_gather(widened, "seq", axis=0, tiled=True),

time: 249 us -> 257 us (1.032); the launches traced: 248 us -> 252 us
    convert_element_type x1, other arithmetic: 2.54 us -> 5.11 us  [shards(): return output.astype(jnp.bfloat16)]
    reshape x0 -> x1, local copies, waits for them, and re-layouts: none -> 2.57 us  [shards(): widened = jnp.concatenate(lax.all_gather(out_weight, 'fsdp'), axis=1)]
    unnamed x32 -> x36, local copies, waits for them, and re-layouts: 10.5 us -> 9.49 us
  transfers between devices with their start and end apart: 10 -> 10, of which waited for: 9 -> 9; matrix products, arithmetic and copies ran while one was open for 27% -> 26% of each run, Pallas kernels for 0% -> 0%
where the time goes in v1:
time: 257 us; the launch traced here: 252 us
  waiting for transfers between devices  136 us (53%)
  matrix products  47 us (18%)
  local copies, waits for them, and re-layouts  24.2 us (9%)
  starting transfers between devices  16.6 us (6%)
  other arithmetic  14.2 us (6%)
  between operations  13.7 us (5%)
    ppermute x8, waiting for transfers between devices, from_behind(): return lax.ppermute(value, axis, pairs)  108 us
    all_gather x1, waiting for transfers between devices, shards(): widened = jnp.concatenate(lax.all_gather(out_weight, 'fsdp'), axis=1)  27.7 us
    dot_general x8, matrix products, attend(): jnp.einsum('gqk,kd->qgd', probs, v_head, preferred_element_type=jnp.float32)  18.8 us
    ppermute x8, starting transfers between devices, from_behind(): return lax.ppermute(value, axis, pairs)  16.6 us
    sub x8, matrix products, attend(): expon = jnp.exp(scores - peak)  15.8 us
    dot_general x1, matrix products, shards(): jnp.dot(attended, lax.all_gather(widened, 'seq', axis=0, tiled=True), pre...  12.4 us
    unnamed x36, local copies, waits for them, and re-layouts  9.49 us
    and x8, other arithmetic, shards(): (q_doc[:, None] == k_doc[None, :]) & (lag >= 0) & (lag < WINDOW_TOKENS)  8.73 us
  transfers between devices with their start and end apart: 10, of which 9 were waited for; matrix products, arithmetic and copies ran while one was open for 26% of the time, Pallas kernels for 0%

profile of v1, /device:TPU:8, one launch (start us, length us, event | category | flops | bytes accessed | tf_op | source)
XLA Modules:
  0.0 252.4 jit_solution(8918355442045091826)
XLA Ops:
  7.3 27.7 %all-gather.6.cloned.1.call-done = bf16[256,2688]{1,0:T(8,128)(2,1)} async-done(((bf16[128,2688]{1,0:T(8,128)(2,1)}), bf16[256,2688]{1,0:T(8,128)(2,1)}) %all-gather.6.cloned.1.call-update) | async-done | bytes 1376272 | tf_op jit(solution)/shard_map/all_gather | solution.py:78
  35.0 2.6 %copy.32 = bf16[128,2,2688]{0,2,1:T(8,128)(2,1)} copy(bf16[128,2,2688]{2,0,1:T(8,128)(2,1)} %bitcast.84) | data formatting | bytes 2752512 | tf_op jit(solution)/shard_map/reshape | solution.py:78
  37.6 2.5 collective-permute-start
  40.3 2.7 %collective-permute-start.4 = (bf16[256,1024]{0,1:T(8,128)(2,1)S(1)}, bf16[256,1024]{0,1:T(8,128)(2,1)S(1)}, u32[]{:S(2)}, u32[]{:S(2)}) collective-permute-start(bf16[256,1024]{0,1:T(8,128)(2,1)S(1)} %copy.28), channel_id=1, source_target_pairs={{0,1},{1,2},{2,3},{3,4},{4,5},{5,6},{6,7},{7,8},{8,9},{9,10},{10,1... | collective-permute-start | bytes 1572872 | tf_op jit(solution)/shard_map/ppermute | solution.py:16
  43.0 12.4 %collective-permute-done = bf16[256,1024]{1,0:T(8,128)(2,1)S(1)} collective-permute-done((bf16[256,1024]{1,0:T(8,128)(2,1)S(1)}, bf16[256,1024]{1,0:T(8,128)(2,1)S(1)}, u32[]{:S(2)}, u32[]{:S(2)}) %collective-permute-start) | collective-permute-done | bytes 524320 | tf_op jit(solution)/shard_map/ppermute | solution.py:16
  55.4 1.9 collective-permute-start.1
  57.3 1.3 copy.30
  58.8 11.5 %collective-permute-done.4 = bf16[256,1024]{0,1:T(8,128)(2,1)S(1)} collective-permute-done((bf16[256,1024]{0,1:T(8,128)(2,1)S(1)}, bf16[256,1024]{0,1:T(8,128)(2,1)S(1)}, u32[]{:S(2)}, u32[]{:S(2)}) %collective-permute-start.4) | collective-permute-done | bytes 524320 | tf_op jit(solution)/shard_map/ppermute | solution.py:16
  70.3 1.9 collective-permute-start.5
  72.2 13.1 %collective-permute-done.1 = bf16[256,1024]{1,0:T(8,128)(2,1)S(1)} collective-permute-done((bf16[256,1024]{1,0:T(8,128)(2,1)S(1)}, bf16[256,1024]{1,0:T(8,128)(2,1)S(1)}, u32[]{:S(2)}, u32[]{:S(2)}) %collective-permute-start.1) | collective-permute-done | bytes 524320 | tf_op jit(solution)/shard_map/ppermute | solution.py:16
  85.4 1.9 collective-permute-start.2
  87.5 14.4 %collective-permute-done.5 = bf16[256,1024]{0,1:T(8,128)(2,1)S(1)} collective-permute-done((bf16[256,1024]{0,1:T(8,128)(2,1)S(1)}, bf16[256,1024]{0,1:T(8,128)(2,1)S(1)}, u32[]{:S(2)}, u32[]{:S(2)}) %collective-permute-start.5) | collective-permute-done | bytes 524320 | tf_op jit(solution)/shard_map/ppermute | solution.py:16
  101.9 1.9 collective-permute-start.6
  103.8 14.9 %collective-permute-done.2 = bf16[256,1024]{1,0:T(8,128)(2,1)S(1)} collective-permute-done((bf16[256,1024]{1,0:T(8,128)(2,1)S(1)}, bf16[256,1024]{1,0:T(8,128)(2,1)S(1)}, u32[]{:S(2)}, u32[]{:S(2)}) %collective-permute-start.2) | collective-permute-done | bytes 524320 | tf_op jit(solution)/shard_map/ppermute | solution.py:16
  118.6 1.9 collective-permute-start.3
  120.6 15.0 %collective-permute-done.6 = bf16[256,1024]{0,1:T(8,128)(2,1)} collective-permute-done((bf16[256,1024]{0,1:T(8,128)(2,1)S(1)}, bf16[256,1024]{0,1:T(8,128)(2,1)}, u32[]{:S(2)}, u32[]{:S(2)}) %collective-permute-start.6) | collective-permute-done | bytes 524320 | tf_op jit(solution)/shard_map/ppermute | solution.py:16
  135.6 1.9 collective-permute-start.7
  137.5 14.8 %collective-permute-done.3 = bf16[256,1024]{1,0:T(8,128)(2,1)S(1)} collective-permute-done((bf16[256,1024]{1,0:T(8,128)(2,1)S(1)}, bf16[256,1024]{1,0:T(8,128)(2,1)S(1)}, u32[]{:S(2)}, u32[]{:S(2)}) %collective-permute-start.3) | collective-permute-done | bytes 524320 | tf_op jit(solution)/shard_map/ppermute | solution.py:16
  152.4 1.1 constant_dynamic-update-slice_fusion.3
  154.7 2.7 %copy.27 = bf16[1280,1024]{0,1:T(8,128)(2,1)} copy(bf16[1280,1024]{1,0:T(8,128)(2,1)S(1)} %constant_dynamic-update-slice_fusion.1) | data formatting | bytes 5242880 | tf_op jit(solution)/shard_map/concatenate | solution.py:37
  157.4 11.9 %collective-permute-done.7 = bf16[256,1024]{0,1:T(8,128)(2,1)} collective-permute-done((bf16[256,1024]{0,1:T(8,128)(2,1)}, bf16[256,1024]{0,1:T(8,128)(2,1)}, u32[]{:S(2)}, u32[]{:S(2)}) %collective-permute-start.7) | collective-permute-done | bytes 524320 | tf_op jit(solution)/shard_map/ppermute | solution.py:16
  169.3 1.9 constant_dynamic-update-slice_fusion.10
  171.2 1.9 constant_dynamic-update-slice_fusion.9
  173.1 2.0 constant_dynamic-update-slice_fusion.8
  176.9 51.1 %while.11 = (s32[]{:T(128)}, bf16[8,256,256]{1,2,0:T(8,128)(2,1)S(1)}, bf16[8,1280,128]{1,2,0:T(8,128)(2,1)}, bf16[8,1280,128]{1,2,0:T(8,128)(2,1)}, bf16[8,256,...) while((s32[]{:T(128)}, ...), condition=%wide.region_6.7_spmd.clone, body=%wide.region_3.6_spmd.clone.sunk | while | flops 511511552 | bytes 2902901 | solution.py:72
  178.9 2.0 fusion.57
  180.8 2.3 fusion.58
  183.2 1.1 fusion.56
  185.2 2.0 fusion.57
  187.2 2.3 fusion.58
  189.6 1.1 fusion.56
  191.6 2.0 fusion.57
  193.6 2.3 fusion.58
  196.0 1.1 fusion.56
  198.0 2.0 fusion.57
  200.0 2.3 fusion.58
  202.4 1.1 fusion.56
  204.4 2.0 fusion.57
  206.4 2.3 fusion.58
  210.8 2.0 fusion.57
  212.8 2.3 fusion.58
  217.2 2.0 fusion.57
  219.2 2.3 fusion.58
  221.6 1.1 fusion.56
  223.6 2.0 fusion.57
  225.6 2.3 fusion.58
  228.0 12.4 %multiply_reduce_fusion = (f32[256]{0:T(256)S(1)}, f32[256,5376]{1,0:T(8,128)}) fusion(bf16[256,2048]{0,1:T(8,128)(2,1)S(1)} %bitcast.85, bf16[2048,5376]{0,1:T(8,128)(2,1)} %all-gather.4.cloned.1.call-done), kind=kOutput, calls=%fused_computation.29 | convolution fusion | flops 5639897088 | bytes 28574720 | tf_op jit(solution)/shard_map/dot_general | solution.py:79
  240.5 5.1 %add_convert_fusion = bf16[256,5376]{1,0:T(8,128)(2,1)} fusion(f32[256,5376]{1,0:T(8,128)} %get-tuple-element.116, bf16[256,5376]{1,0:T(8,128)(2,1)S(1)} %copy-done, f32[256]{0:T(256)S(1)} %add_rsqrt_fusion, f32[5376]{0:T(1024)S(1)} %copy-done.10), kind=kLoop, calls=%fused_computation.28 | loop fusion | flops 6881280 | bytes 11032576 | tf_op jit(solution)/shard_map/convert_element_type | solution.py:86
  (68 shorter events, 15.1 us)
Async XLA Ops:
  6.5 31.1 %copy-start.3 = (bf16[256,1024]{1,0:T(8,128)(2,1)S(1)}, bf16[256,1024]{1,0:T(8,128)(2,1)}, u32[]{:S(2)}) copy-start(bf16[256,1024]{1,0:T(8,128)(2,1)} %param.11) | copy-start | bytes 1572868
  6.5 33.6 %copy-start.2 = (bf16[256,1024]{1,0:T(8,128)(2,1)S(1)}, bf16[256,1024]{1,0:T(8,128)(2,1)}, u32[]{:S(2)}) copy-start(bf16[256,1024]{1,0:T(8,128)(2,1)} %param.10) | copy-start | bytes 1572868
  6.5 28.5 %all-gather.6.cloned.1.call-start = ((), (), s32[]{:S(2)}) async-start(), calls=%async_computation.1 | async-start | bytes 2064384 | tf_op jit(solution)/shard_map/all_gather | solution.py:78
  7.3 50.1 %copy-start.1 = (bf16[256,2048]{1,0:T(8,128)(2,1)S(1)}, bf16[256,2048]{1,0:T(8,128)(2,1)}, u32[]{:S(2)}) copy-start(bf16[256,2048]{1,0:T(8,128)(2,1)} %param.9) | copy-start | bytes 3145732
  7.3 220.7 %all-gather.4.cloned.1.call-start = ((), (), s32[]{:S(2)}) async-start(), calls=%async_computation | async-start | bytes 23396352 | tf_op jit(solution)/shard_map/all_gather | solution.py:81
  37.6 21.0 %copy-start.12 = (s32[8]{0:T(128)S(1)}, s32[8]{0:T(128)}, u32[]{:S(2)}) copy-start(s32[8]{0:T(128)} %param.15) | copy-start | bytes 100
  37.6 17.7 %collective-permute-start = (bf16[256,1024]{1,0:T(8,128)(2,1)S(1)}, bf16[256,1024]{1,0:T(8,128)(2,1)S(1)}, u32[]{:S(2)}, u32[]{:S(2)}) collective-permute-start(bf16[256,1024]{1,0:T(8,128)(2,1)S(1)} %copy-done.3), channel_id=1, source_target_pairs={{0,1},{1,2},{2,3},{3,4},{4,5},{5,6},{6,7},{7,8},{8,9},{9,10},{10,1... | collective-permute-start | bytes 1572872 | tf_op jit(solution)/shard_map/ppermute | solution.py:16
  40.3 30.0 %collective-permute-start.4 = (bf16[256,1024]{0,1:T(8,128)(2,1)S(1)}, bf16[256,1024]{0,1:T(8,128)(2,1)S(1)}, u32[]{:S(2)}, u32[]{:S(2)}) collective-permute-start(bf16[256,1024]{0,1:T(8,128)(2,1)S(1)} %copy.28), channel_id=1, source_target_pairs={{0,1},{1,2},{2,3},{3,4},{4,5},{5,6},{6,7},{7,8},{8,9},{9,10},{10,1... | collective-permute-start | bytes 1572872 | tf_op jit(solution)/shard_map/ppermute | solution.py:16
  55.4 82.1 %copy-start.6 = (bf16[256,1024]{1,0:T(8,128)(2,1)}, bf16[256,1024]{1,0:T(8,128)(2,1)S(1)}, u32[]{:S(2)}) copy-start(bf16[256,1024]{1,0:T(8,128)(2,1)S(1)} %collective-permute-done) | copy-start | bytes 1572868
  55.4 30.0 %collective-permute-start.1 = (bf16[256,1024]{1,0:T(8,128)(2,1)S(1)}, bf16[256,1024]{1,0:T(8,128)(2,1)S(1)}, u32[]{:S(2)}, u32[]{:S(2)}) collective-permute-start(bf16[256,1024]{1,0:T(8,128)(2,1)S(1)} %collective-permute-done), channel_id=1, source_target_pairs={{0,1},{1,2},{2,3},{3,4},{4,5},{5,6},{6,7},{7,8},{8,9},{9,10},{10,1... | collective-permute-start | bytes 1572872 | tf_op jit(solution)/shard_map/ppermute | solution.py:16
  70.3 67.2 %copy-start.4 = (bf16[256,1024]{0,1:T(8,128)(2,1)}, bf16[256,1024]{0,1:T(8,128)(2,1)S(1)}, u32[]{:S(2)}) copy-start(bf16[256,1024]{0,1:T(8,128)(2,1)S(1)} %collective-permute-done.4) | copy-start | bytes 1572868
  70.3 31.5 %collective-permute-start.5 = (bf16[256,1024]{0,1:T(8,128)(2,1)S(1)}, bf16[256,1024]{0,1:T(8,128)(2,1)S(1)}, u32[]{:S(2)}, u32[]{:S(2)}) collective-permute-start(bf16[256,1024]{0,1:T(8,128)(2,1)S(1)} %collective-permute-done.4), channel_id=1, source_target_pairs={{0,1},{1,2},{2,3},{3,4},{4,5},{5,6},{6,7},{7,8},{8,9},{9,10},{10,1... | collective-permute-start | bytes 1572872 | tf_op jit(solution)/shard_map/ppermute | solution.py:16
  85.4 52.2 %copy-start.8 = (bf16[256,1024]{1,0:T(8,128)(2,1)}, bf16[256,1024]{1,0:T(8,128)(2,1)S(1)}, u32[]{:S(2)}) copy-start(bf16[256,1024]{1,0:T(8,128)(2,1)S(1)} %collective-permute-done.1) | copy-start | bytes 1572868
  85.4 33.3 %collective-permute-start.2 = (bf16[256,1024]{1,0:T(8,128)(2,1)S(1)}, bf16[256,1024]{1,0:T(8,128)(2,1)S(1)}, u32[]{:S(2)}, u32[]{:S(2)}) collective-permute-start(bf16[256,1024]{1,0:T(8,128)(2,1)S(1)} %collective-permute-done.1), channel_id=1, source_target_pairs={{0,1},{1,2},{2,3},{3,4},{4,5},{5,6},{6,7},{7,8},{8,9},{9,10},{10,1... | collective-permute-start | bytes 1572872 | tf_op jit(solution)/shard_map/ppermute | solution.py:16
  101.9 35.7 %copy-start.9 = (bf16[256,1024]{0,1:T(8,128)(2,1)}, bf16[256,1024]{0,1:T(8,128)(2,1)S(1)}, u32[]{:S(2)}) copy-start(bf16[256,1024]{0,1:T(8,128)(2,1)S(1)} %collective-permute-done.5) | copy-start | bytes 1572868
  101.9 33.7 %collective-permute-start.6 = (bf16[256,1024]{0,1:T(8,128)(2,1)S(1)}, bf16[256,1024]{0,1:T(8,128)(2,1)}, u32[]{:S(2)}, u32[]{:S(2)}) collective-permute-start(bf16[256,1024]{0,1:T(8,128)(2,1)S(1)} %collective-permute-done.5), channel_id=1, source_target_pairs={{0,1},{1,2},{2,3},{3,4},{4,5},{5,6},{6,7},{7,8},{8,9},{9,10},{10,1... | collective-permute-start | bytes 1572872 | tf_op jit(solution)/shard_map/ppermute | solution.py:16
  118.6 33.7 %collective-permute-start.3 = (bf16[256,1024]{1,0:T(8,128)(2,1)S(1)}, bf16[256,1024]{1,0:T(8,128)(2,1)S(1)}, u32[]{:S(2)}, u32[]{:S(2)}) collective-permute-start(bf16[256,1024]{1,0:T(8,128)(2,1)S(1)} %collective-permute-done.2), channel_id=1, source_target_pairs={{0,1},{1,2},{2,3},{3,4},{4,5},{5,6},{6,7},{7,8},{8,9},{9,10},{10,1... | collective-permute-start | bytes 1572872 | tf_op jit(solution)/shard_map/ppermute | solution.py:16
  135.6 33.7 %collective-permute-start.7 = (bf16[256,1024]{0,1:T(8,128)(2,1)}, bf16[256,1024]{0,1:T(8,128)(2,1)}, u32[]{:S(2)}, u32[]{:S(2)}) collective-permute-start(bf16[256,1024]{0,1:T(8,128)(2,1)} %collective-permute-done.6), channel_id=1, source_target_pairs={{0,1},{1,2},{2,3},{3,4},{4,5},{5,6},{6,7},{7,8},{8,9},{9,10},{10,1... | collective-permute-start | bytes 1572872 | tf_op jit(solution)/shard_map/ppermute | solution.py:16
  152.3 1.2 copy-start.7
  157.3 17.7 %copy-start.5 = (bf16[256,1024]{0,1:T(8,128)(2,1)S(1)}, bf16[256,1024]{0,1:T(8,128)(2,1)}, u32[]{:S(2)}) copy-start(bf16[256,1024]{0,1:T(8,128)(2,1)} %copy-done.4) | copy-start | bytes 1572868
  157.4 19.5 %copy-start.11 = (bf16[8,256,256]{1,2,0:T(8,128)(2,1)S(1)}, bf16[8,256,256]{1,2,0:T(8,128)(2,1)}, u32[]{:S(2)}) copy-start(bf16[8,256,256]{1,2,0:T(8,128)(2,1)} %custom-call.2) | copy-start | bytes 3145732
  228.0 12.5 %copy-start = (bf16[256,5376]{1,0:T(8,128)(2,1)S(1)}, bf16[256,5376]{1,0:T(8,128)(2,1)}, u32[]{:S(2)}) copy-start(bf16[256,5376]{1,0:T(8,128)(2,1)} %param.13) | copy-start | bytes 8257540
  228.0 12.5 %copy-start.10 = (f32[5376]{0:T(1024)S(1)}, f32[5376]{0:T(1024)}, u32[]{:S(2)}) copy-start(f32[5376]{0:T(1024)} %param.14) | copy-start | bytes 64516
Sparse Core Ops, SparseCore 0:
  8.9 26.1 all-gather.5
  37.8 119.6 all-gather.3
